TPU v7x, 32 devices: a whole 2x2x4 slice. The times are simulated.
32 devices in a mesh: band: 16 (over z, y, core), ga: 2 (over x).
Axes of the slice: x: 2, y: 2, z: 4, core: 2. Of those that a mesh axis runs over, the one named last changes fastest.
Arguments:
- orbitals: bfloat16 [2, 16, 160, 128], P(None, 'band', 'ga'), may hold values from -8 to 8, as said below
- potential: float32 [480, 480], P('ga'), may hold values from -2 to 2
- slot_sticks: int32 [160], replicated, may hold values from -1 to 126, as said below
- stick_entries: int32 [160, 128], replicated, may hold values from -1 to 126, as said below
Outputs:
- applied_orbitals: bfloat16 [2, 16, 160, 128], P(None, 'band', 'ga')
- correlation: float32 [2, 16, 16], replicated
- reduced_hamiltonian: float32 [2, 16, 16], replicated
Inputs may be any that keep to these rules, and one draw needn't show every extreme that they name: `slot_sticks`: every gx with |gx| < 64 is held by exactly one slot; the other slots hold -1. Slots t with t // 80 = d are those of index d of ga; on some index of ga all 80 slots hold sticks. `stick_entries`: row t lists, in some order, gz + 63 for every gz with gx^2 + gz^2 < 64^2, gx being the stick of slot t, then -1 to the end of the row; rows of empty slots are all -1. `orbitals`: entries where stick_entries is -1 carry values that are not used.
All inputs are finite; a program needn't handle non-finite values.
Results may differ from a plain program's by a relative error of at most 0.001.
Values may be sent and summed in bfloat16 or wider, within the bound.
A program may use at most 64 MiB of HBM per device.

v0:
```python
import jax
import jax.numpy as jnp
from jax import lax
from jax.sharding import PartitionSpec as P

TWO_PI = 6.283185307179586
HIGHEST_PRECISION = lax.Precision.HIGHEST


def phases(frequency, position, points):
    winding = frequency[:, None] * position[None, :] % points
    angles = winding.astype(jnp.float32) * (TWO_PI / points)
    return (jnp.cos(angles), jnp.sin(angles))


def stick_phases(slot_sticks, radius, points):
    frequency = slot_sticks - radius + 1
    x_cos, x_sin = phases(frequency, jnp.arange(points, dtype=jnp.int32), points)
    filled = (slot_sticks >= 0).astype(jnp.float32)[:, None]
    return (x_cos * filled, x_sin * filled)


def selector_table(entry_lists):
    width = entry_lists.shape[1]
    return (entry_lists[:, :, None] == jnp.arange(width, dtype=jnp.int32)[None, None, :]).astype(
        jnp.bfloat16
    )


def spread_entries(coeffs, selector):
    return jnp.einsum("cbsk,skp->cbsp", coeffs, selector, preferred_element_type=jnp.float32)


def pick_entries(spectra, selector):
    return jnp.einsum(
        "cbsp,skp->cbsk", spectra, selector.astype(jnp.float32), precision=HIGHEST_PRECISION
    )


def z_forward(spread, z_cos, z_sin):
    real_part = jnp.einsum(
        "bsp,pz->bsz", spread[0], z_cos, precision=HIGHEST_PRECISION
    ) - jnp.einsum("bsp,pz->bsz", spread[1], z_sin, precision=HIGHEST_PRECISION)
    imag_part = jnp.einsum(
        "bsp,pz->bsz", spread[0], z_sin, precision=HIGHEST_PRECISION
    ) + jnp.einsum("bsp,pz->bsz", spread[1], z_cos, precision=HIGHEST_PRECISION)
    return jnp.stack([real_part, imag_part])


def plane_work(columns, x_cos, x_sin, potential):
    field_real = jnp.einsum(
        "bsz,sx->bzx", columns[0], x_cos, precision=HIGHEST_PRECISION
    ) - jnp.einsum("bsz,sx->bzx", columns[1], x_sin, precision=HIGHEST_PRECISION)
    field_imag = jnp.einsum(
        "bsz,sx->bzx", columns[0], x_sin, precision=HIGHEST_PRECISION
    ) + jnp.einsum("bsz,sx->bzx", columns[1], x_cos, precision=HIGHEST_PRECISION)
    prod_real = potential[None] * field_real
    prod_imag = potential[None] * field_imag
    back_real = jnp.einsum(
        "bzx,sx->bsz", prod_real, x_cos, precision=HIGHEST_PRECISION
    ) + jnp.einsum("bzx,sx->bsz", prod_imag, x_sin, precision=HIGHEST_PRECISION)
    back_imag = jnp.einsum(
        "bzx,sx->bsz", prod_imag, x_cos, precision=HIGHEST_PRECISION
    ) - jnp.einsum("bzx,sx->bsz", prod_real, x_sin, precision=HIGHEST_PRECISION)
    return jnp.stack([back_real, back_imag])


def z_backward(gathered, z_cos, z_sin, points):
    real_part = jnp.einsum(
        "bsz,pz->bsp", gathered[0], z_cos, precision=HIGHEST_PRECISION
    ) + jnp.einsum("bsz,pz->bsp", gathered[1], z_sin, precision=HIGHEST_PRECISION)
    imag_part = jnp.einsum(
        "bsz,pz->bsp", gathered[1], z_cos, precision=HIGHEST_PRECISION
    ) - jnp.einsum("bsz,pz->bsp", gathered[0], z_sin, precision=HIGHEST_PRECISION)
    return jnp.stack([real_part, imag_part]) / float(points * points)


def kinetic_factor(sticks, entry_lists, radius):
    gx_value = sticks - radius + 1
    gz_value = entry_lists - radius + 1
    return ((gx_value * gx_value)[:, None] + gz_value * gz_value).astype(jnp.float32) / float(
        radius * radius
    )


def cross_products(left, right, scale):
    dims = (((1,), (1,)), ((), ()))
    real_part = lax.dot_general(
        left[0], right[0], dims, preferred_element_type=jnp.float32
    ) + lax.dot_general(left[1], right[1], dims, preferred_element_type=jnp.float32)
    imag_part = lax.dot_general(
        left[0], right[1], dims, preferred_element_type=jnp.float32
    ) - lax.dot_general(left[1], right[0], dims, preferred_element_type=jnp.float32)
    return jnp.stack([real_part, imag_part]) * scale


def body(orbitals, potential, slot_sticks, stick_entries):
    points = potential.shape[1]
    width = stick_entries.shape[1]
    radius = width // 2
    band_count = orbitals.shape[1]
    slot_count = orbitals.shape[2]
    ga_index = lax.axis_index("ga")
    own_first = ga_index * slot_count
    own_lists = lax.dynamic_slice_in_dim(stick_entries, own_first, slot_count, 0)
    own_sticks = lax.dynamic_slice_in_dim(slot_sticks, own_first, slot_count, 0)
    present = own_lists >= 0
    own_selector = selector_table(own_lists)
    masked = jnp.where(present[None, None], orbitals, jnp.zeros_like(orbitals))
    frequency = jnp.arange(width, dtype=jnp.int32) - radius + 1
    whole_cos, whole_sin = phases(frequency, jnp.arange(points, dtype=jnp.int32), points)
    x_cos, x_sin = stick_phases(slot_sticks, radius, points)
    columns = z_forward(spread_entries(orbitals, own_selector), whole_cos, whole_sin)
    planes_columns = lax.all_to_all(columns, "ga", split_axis=3, concat_axis=2, tiled=True)
    gathered = plane_work(planes_columns, x_cos, x_sin, potential)
    returned = lax.all_to_all(gathered, "ga", split_axis=2, concat_axis=3, tiled=True)
    spectra = z_backward(returned, whole_cos, whole_sin, points)
    applied = pick_entries(spectra, own_selector)
    kinetic = kinetic_factor(own_sticks, own_lists, radius)
    applied_orbitals = jnp.where(
        present[None, None],
        kinetic[None, None] * orbitals.astype(jnp.float32) + applied,
        jnp.float32(0.0),
    ).astype(jnp.bfloat16)
    scale = 1.0 / (4.0 * radius * radius)
    flat_psi = masked.reshape(2, band_count, -1)
    flat_h = applied_orbitals.reshape(2, band_count, -1)
    portion = lax.all_gather(masked, "band", axis=1, tiled=True)
    remote_psi = portion.reshape(2, portion.shape[1], -1)
    block = jnp.stack(
        [cross_products(remote_psi, flat_psi, scale), cross_products(remote_psi, flat_h, scale)]
    )
    summed = lax.psum(block, "ga")
    matrices = lax.all_gather(summed, "band", axis=3, tiled=True)
    return (applied_orbitals, matrices[0], matrices[1])


def solution(mesh):
    return jax.shard_map(
        body,
        mesh=mesh,
        in_specs=(P(None, "band", "ga", None), P("ga", None), P(), P()),
        out_specs=(P(None, "band", "ga", None), P(), P()),
        check_vma=False,
    )
```

profile of v0, /device:TPU:0, one launch (start us, length us, event | category | flops | bytes accessed | tf_op | source)
XLA Modules:
  0.0 106.6 jit_solution(10663238395581667539)
XLA Ops:
  2.3 3.0 %fusion.10 = f32[2,1,80,128]{3,0,2,1:T(2,128)S(1)} fusion(s32[80,128]{1,0:T(8,128)S(1)} %get-tuple-element.16, bf16[2,80,128]{2,1,0:T(8,128)(2,1)} %bitcast.158), kind=kOutput, calls=%fused_computation.17 | convolution fusion | flops 6553600 | bytes 163840 | tf_op jit(solution)/shard_map/cbsk,skp->cbsp/dot_general | solution.py:31
  5.3 1.3 %fusion.53 = f32[80,480]{1,0:T(8,128)S(1)} fusion(f32[80,128]{1,0:T(8,128)S(1)} %bitcast.156, s32[128]{0:T(128)S(1)} %iota_add_fusion), kind=kOutput, calls=%fused_computation.76 | convolution fusion | flops 59535360 | bytes 195072 | tf_op jit(solution)/shard_map/bsp,pz->bsz/dot_general | solution.py:41
  6.7 1.4 %fusion.57 = f32[80,480]{1,0:T(8,128)S(1)} fusion(f32[80,128]{1,0:T(8,128)S(1)} %bitcast.157, s32[128]{0:T(128)S(1)} %iota_add_fusion), kind=kOutput, calls=%fused_computation.77 | convolution fusion | flops 59535360 | bytes 195072 | tf_op jit(solution)/shard_map/bsp,pz->bsz/dot_general | solution.py:44
  8.1 1.4 %fusion.9 = f32[1,1,80,480]{3,2,1,0:T(8,128)S(1)} fusion(f32[80,480]{1,0:T(8,128)S(1)} %fusion.53, f32[80,128]{1,0:T(8,128)S(1)} %bitcast.154, s32[128]{0:T(128)S(1)} %iota_add_fusion), kind=kOutput, calls=%fused_computation.16 | convolution fusion | flops 59573760 | bytes 348672 | tf_op jit(solution)/shard_map/bsp,pz->bsz/dot_general | solution.py:43
  9.5 1.4 %fusion.8 = f32[1,1,80,480]{3,2,1,0:T(8,128)S(1)} fusion(f32[80,480]{1,0:T(8,128)S(1)} %fusion.57, f32[80,128]{1,0:T(8,128)S(1)} %bitcast.155, s32[128]{0:T(128)S(1)} %iota_add_fusion), kind=kOutput, calls=%fused_computation.14 | convolution fusion | flops 59573760 | bytes 348672 | tf_op jit(solution)/shard_map/bsp,pz->bsz/dot_general | solution.py:46
  11.9 4.4 %all-to-all-start = ((f32[2,1,80,480]{2,1,0,3:T(1,128)}), f32[2,1,80,480]{2,1,0,3:T(1,128)S(1)}, u32[]{:S(2)}, u32[]{:S(2)}) async-start(f32[2,1,80,480]{2,1,0,3:T(1,128)} %copy.37), calls=%async_computation | async-start | bytes 983040 | tf_op jit(solution)/shard_map/all_to_all | solution.py:114
  16.4 24.4 %all_gather.6 = bf16[2,16,80,128]{3,2,0,1:T(8,128)(2,1)S(1)} all-gather(bf16[2,1,80,128]{3,2,0,1:T(8,128)(2,1)S(1)} %copy.45), channel_id=1, replica_groups=mesh['band'=16,'ga'=2] {'band'}, dimensions={1}, use_global_device_ids=true | all-gather | bytes 696320 | tf_op jit(solution)/shard_map/all_gather | solution.py:128
  42.3 1.9 %fusion.40 = f32[240,480]{1,0:T(8,128)S(1)} fusion(f32[160,240]{1,0:T(8,128)S(1)} %bitcast.152, f32[160]{0:T(256)S(1)} %compare_convert_fusion, s32[160]{0:T(256)S(1)} %broadcast_add_fusion), kind=kOutput, calls=%fused_computation.65 | convolution fusion | flops 221952000 | bytes 615680 | tf_op jit(solution)/shard_map/bsz,sx->bzx/dot_general | solution.py:51
  44.2 1.9 %fusion.41 = f32[240,480]{1,0:T(8,128)S(1)} fusion(f32[160,240]{1,0:T(8,128)S(1)} %bitcast.153, f32[160]{0:T(256)S(1)} %compare_convert_fusion, s32[160]{0:T(256)S(1)} %broadcast_add_fusion), kind=kOutput, calls=%fused_computation.66 | convolution fusion | flops 221952000 | bytes 615680 | tf_op jit(solution)/shard_map/bsz,sx->bzx/dot_general | solution.py:54
  46.1 1.9 %fusion.5 = f32[240,480]{1,0:T(8,128)S(1)} fusion(f32[240,480]{1,0:T(8,128)S(1)} %copy-done, f32[240,480]{1,0:T(8,128)S(1)} %fusion.40, f32[160,240]{1,0:T(8,128)S(1)} %bitcast.139, f32[160]{0:T(256)S(1)} %compare_convert_fusion, s32[160]{0:T(256)S(1)} %broadcast_add_fusion), kind=kOutput, calls=%fused_computation.8 | convolution fusion | flops 222182400 | bytes 1537280 | tf_op jit(solution)/shard_map/bsz,sx->bzx/dot_general | solution.py:53
  48.0 1.9 %fusion.39 = f32[160,240]{1,0:T(8,128)S(1)} fusion(f32[240,480]{1,0:T(8,128)S(1)} %fusion.5, f32[160]{0:T(256)S(1)} %compare_convert_fusion, s32[160]{0:T(256)S(1)} %broadcast_add_fusion), kind=kOutput, calls=%fused_computation.64 | convolution fusion | flops 221952000 | bytes 615680 | tf_op jit(solution)/shard_map/bzx,sx->bsz/dot_general | solution.py:59
  49.9 1.9 %fusion.4 = f32[240,480]{1,0:T(8,128)S(1)} fusion(f32[240,480]{1,0:T(8,128)S(1)} %copy-done, f32[240,480]{1,0:T(8,128)S(1)} %fusion.41, f32[160,240]{1,0:T(8,128)S(1)} %bitcast.140, f32[160]{0:T(256)S(1)} %compare_convert_fusion, s32[160]{0:T(256)S(1)} %broadcast_add_fusion), kind=kOutput, calls=%fused_computation.6 | convolution fusion | flops 222182400 | bytes 1537280 | tf_op jit(solution)/shard_map/bsz,sx->bzx/dot_general | solution.py:56
  51.8 1.9 %fusion.38 = f32[160,240]{1,0:T(8,128)S(1)} fusion(f32[240,480]{1,0:T(8,128)S(1)} %fusion.4, f32[160]{0:T(256)S(1)} %compare_convert_fusion, s32[160]{0:T(256)S(1)} %broadcast_add_fusion), kind=kOutput, calls=%fused_computation.63 | convolution fusion | flops 221952000 | bytes 615680 | tf_op jit(solution)/shard_map/bzx,sx->bsz/dot_general | solution.py:62
  53.7 2.1 %fusion.7 = f32[1,1,160,240]{3,2,1,0:T(8,128)S(1)} fusion(f32[160,240]{1,0:T(8,128)S(1)} %fusion.39, f32[240,480]{1,0:T(8,128)S(1)} %fusion.4, f32[160]{0:T(256)S(1)} %compare_convert_fusion, s32[160]{0:T(256)S(1)} %broadcast_add_fusion), kind=kOutput, calls=%fused_computation.12 | convolution fusion | flops 221990400 | bytes 769280 | tf_op jit(solution)/shard_map/bzx,sx->bsz/dot_general | solution.py:61
  55.9 1.9 %fusion.6 = f32[1,1,160,240]{3,2,1,0:T(8,128)S(1)} fusion(f32[160,240]{1,0:T(8,128)S(1)} %fusion.38, f32[240,480]{1,0:T(8,128)S(1)} %fusion.5, f32[160]{0:T(256)S(1)} %compare_convert_fusion, s32[160]{0:T(256)S(1)} %broadcast_add_fusion), kind=kOutput, calls=%fused_computation.10 | convolution fusion | flops 221990400 | bytes 769280 | tf_op jit(solution)/shard_map/bzx,sx->bsz/dot_general | solution.py:64
  58.9 3.5 %all-to-all-start.1 = ((f32[2,1,160,240]{3,1,0,2:T(1,128)}), f32[2,1,160,240]{3,1,0,2:T(1,128)S(1)}, u32[]{:S(2)}, u32[]{:S(2)}) async-start(f32[2,1,160,240]{3,1,0,2:T(1,128)} %copy.41), calls=%async_computation.1 | async-start | bytes 655360 | tf_op jit(solution)/shard_map/all_to_all | solution.py:116
  62.8 6.5 %all-to-all-done.1 = f32[2,1,160,240]{3,1,0,2:T(1,128)S(1)} async-done(((f32[2,1,160,240]{3,1,0,2:T(1,128)}), f32[2,1,160,240]{3,1,0,2:T(1,128)S(1)}, u32[]{:S(2)}, u32[]{:S(2)}) %all-to-all-start.1) | async-done | bytes 307232 | tf_op jit(solution)/shard_map/all_to_all | solution.py:116
  70.0 1.4 %fusion.50 = f32[80,128]{1,0:T(8,128)S(1)} fusion(f32[80,480]{1,0:T(8,128)S(1)} %reshape.267, s32[128]{0:T(128)S(1)} %iota_add_fusion), kind=kOutput, calls=%fused_computation.75 | convolution fusion | flops 59535360 | bytes 195072 | tf_op jit(solution)/shard_map/bsz,pz->bsp/dot_general | solution.py:69
  71.6 1.4 %fusion.48 = f32[80,128]{1,0:T(8,128)S(1)} fusion(f32[80,480]{1,0:T(8,128)S(1)} %reshape.268, s32[128]{0:T(128)S(1)} %iota_add_fusion), kind=kOutput, calls=%fused_computation.74 | convolution fusion | flops 59535360 | bytes 195072 | tf_op jit(solution)/shard_map/bsz,pz->bsp/dot_general | solution.py:72
  73.0 1.4 %fusion.16 = f32[1,80,128]{2,1,0:T(8,128)S(1)} fusion(f32[80,128]{1,0:T(8,128)S(1)} %fusion.50, f32[80,480]{1,0:T(8,128)S(1)} %reshape.268, s32[128]{0:T(128)S(1)} %iota_add_fusion), kind=kOutput, calls=%fused_computation.25 | convolution fusion | flops 59545600 | bytes 236032 | tf_op jit(solution)/shard_map/bsz,pz->bsp/dot_general | solution.py:71
  74.5 1.5 %fusion.15 = f32[1,80,128]{2,1,0:T(8,128)S(1)} fusion(f32[80,128]{1,0:T(8,128)S(1)} %fusion.48, f32[80,480]{1,0:T(8,128)S(1)} %reshape.267, s32[128]{0:T(128)S(1)} %iota_add_fusion), kind=kOutput, calls=%fused_computation.23 | convolution fusion | flops 59545600 | bytes 236032 | tf_op jit(solution)/shard_map/bsz,pz->bsp/dot_general | solution.py:74
  76.0 5.6 %fusion.14 = bf16[2,1,80,128]{3,0,2,1:T(2,128)(2,1)S(1)} fusion(s32[80,128]{1,0:T(8,128)S(1)} %get-tuple-element.16, f32[2,80,128]{2,1,0:T(8,128)S(1)} %maximum_multiply_fusion, pred[80,128]{1,0:T(8,128)(4,1)S(1)} %broadcast_compare_fusion, f32[80,128]{1,0:T(8,128)S(1)} %get-tuple-element.15, bf16[2,1,80,128]{3,2,1,0:T(8,128)(2,1)S(1)} %copy-done.1), kind=kOutput, calls=%fused_computation.21 | convolution fusion | flops 32870400 | bytes 256000 | tf_op jit(solution)/shard_map/cbsp,skp->cbsk/dot_general | solution.py:35
  83.1 4.9 %psum.7 = f32[2,2,16,1]{2,3,1,0:T(1,128)S(1)} all-reduce(f32[2,2,16,1]{2,3,1,0:T(1,128)S(1)} %pad_maximum_fusion.2), channel_id=1, replica_groups=mesh['band'=16,'ga'=2] {'ga'}, use_global_device_ids=true, to_apply=%region_0.1 | all-reduce | flops 64 | bytes 512 | tf_op jit(solution)/shard_map/psum | solution.py:133
  88.1 17.2 %all_gather.7 = f32[2,2,16,16]{2,1,0,3:T(2,128)S(1)} all-gather(f32[2,2,16,1]{2,1,0,3:T(2,128)S(1)} %bitcast.159), channel_id=1, replica_groups=mesh['band'=16,'ga'=2] {'band'}, dimensions={3}, use_global_device_ids=true | all-gather | bytes 4352 | tf_op jit(solution)/shard_map/all_gather | solution.py:134
  (45 shorter events, 9.7 us)
Async XLA Ops:
  11.9 4.4 %copy-start.2 = (s32[160]{0:T(256)S(1)}, s32[160]{0:T(256)}, u32[]{:S(2)}) copy-start(s32[160]{0:T(256)} %param.6) | copy-start | bytes 1924
  11.9 4.4 %copy-start.1 = (bf16[2,1,80,128]{3,2,1,0:T(8,128)(2,1)S(1)}, bf16[2,1,80,128]{3,2,1,0:T(8,128)(2,1)}, u32[]{:S(2)}) copy-start(bf16[2,1,80,128]{3,2,1,0:T(8,128)(2,1)} %param.4) | copy-start | bytes 122884
  11.9 29.4 %all-to-all-start = ((f32[2,1,80,480]{2,1,0,3:T(1,128)}), f32[2,1,80,480]{2,1,0,3:T(1,128)S(1)}, u32[]{:S(2)}, u32[]{:S(2)}) async-start(f32[2,1,80,480]{2,1,0,3:T(1,128)} %copy.37), calls=%async_computation | async-start | bytes 983040 | tf_op jit(solution)/shard_map/all_to_all | solution.py:114
  44.2 1.9 %copy-start = (f32[240,480]{1,0:T(8,128)S(1)}, f32[240,480]{1,0:T(8,128)}, u32[]{:S(2)}) copy-start(f32[240,480]{1,0:T(8,128)} %param.5) | copy-start | bytes 1382404
  58.9 10.4 %all-to-all-start.1 = ((f32[2,1,160,240]{3,1,0,2:T(1,128)}), f32[2,1,160,240]{3,1,0,2:T(1,128)S(1)}, u32[]{:S(2)}, u32[]{:S(2)}) async-start(f32[2,1,160,240]{3,1,0,2:T(1,128)} %copy.41), calls=%async_computation.1 | async-start | bytes 655360 | tf_op jit(solution)/shard_map/all_to_all | solution.py:116
where the time goes:
time: 107 us
  blocking collectives  46.5 us (43%)
  matrix products  37 us (35%)
  starting transfers between devices  7.82 us (7%)
  waiting for transfers between devices  6.46 us (6%)
  local copies, waits for them, and re-layouts  6.1 us (6%)
  other arithmetic  1.8 us (2%)
    all_gather x1, blocking collectives, body(): portion = lax.all_gather(masked, 'band', axis=1, tiled=True)  24.4 us
    all_gather x1, blocking collectives, body(): matrices = lax.all_gather(summed, 'band', axis=3, tiled=True)  17.2 us
    all_to_all x1, waiting for transfers between devices, body(): lax.all_to_all(gathered, 'ga', split_axis=2, concat_axis=3, tiled=True)  6.46 us
    dot_general x1, matrix products, pick_entries(): jnp.einsum('cbsp,skp->cbsk', spectra, selector.astype(jnp.float32), preci...  5.62 us
    psum x1, blocking collectives, body(): summed = lax.psum(block, 'ga')  4.93 us
    all_to_all x1, starting transfers between devices, body(): lax.all_to_all(columns, 'ga', split_axis=3, concat_axis=2, tiled=True)  4.36 us
    all_to_all x1, starting transfers between devices, body(): lax.all_to_all(gathered, 'ga', split_axis=2, concat_axis=3, tiled=True)  3.45 us
    dot_general x1, matrix products, spread_entries(): jnp.einsum('cbsk,skp->cbsp', coeffs, selector, preferred_element_type=jnp...  3.01 us
  transfers between devices with their start and end apart: 2, of which 1 were waited for; matrix products, arithmetic and copies ran while one was open for 1% of the time, Pallas kernels for 0%

commit v1 on v0

--- a/solution.py
+++ b/solution.py
@@ -125,7 +125,8 @@
     scale = 1.0 / (4.0 * radius * radius)
     flat_psi = masked.reshape(2, band_count, -1)
     flat_h = applied_orbitals.reshape(2, band_count, -1)
-    portion = lax.all_gather(masked, "band", axis=1, tiled=True)
+    shards = lax.all_gather(masked, "band", axis=0, tiled=False)
+    portion = jnp.concatenate(shards, axis=1)
     remote_psi = portion.reshape(2, portion.shape[1], -1)
     block = jnp.stack(
         [cross_products(remote_psi, flat_psi, scale), cross_products(remote_psi, flat_h, scale)]

time: 107 us -> 107 us (level)
  no operation moved by 1% of the time
where the time goes in v1:
time: 107 us
  blocking collectives  46.5 us (43%)
  matrix products  37 us (35%)
  starting transfers between devices  7.82 us (7%)
  waiting for transfers between devices  6.46 us (6%)
  local copies, waits for them, and re-layouts  6.1 us (6%)
  other arithmetic  1.8 us (2%)
    all_gather x1, blocking collectives, body(): shards = lax.all_gather(masked, 'band', axis=0, tiled=False)  24.4 us
    all_gather x1, blocking collectives, body(): matrices = lax.all_gather(summed, 'band', axis=3, tiled=True)  17.2 us
    all_to_all x1, waiting for transfers between devices, body(): lax.all_to_all(gathered, 'ga', split_axis=2, concat_axis=3, tiled=True)  6.46 us
    dot_general x1, matrix products, pick_entries(): jnp.einsum('cbsp,skp->cbsk', spectra, selector.astype(jnp.float32), preci...  5.62 us
    psum x1, blocking collectives, body(): summed = lax.psum(block, 'ga')  4.93 us
    all_to_all x1, starting transfers between devices, body(): lax.all_to_all(columns, 'ga', split_axis=3, concat_axis=2, tiled=True)  4.36 us
    all_to_all x1, starting transfers between devices, body(): lax.all_to_all(gathered, 'ga', split_axis=2, concat_axis=3, tiled=True)  3.45 us
    dot_general x1, matrix products, spread_entries(): jnp.einsum('cbsk,skp->cbsp', coeffs, selector, preferred_element_type=jnp...  3.01 us
  transfers between devices with their start and end apart: 2, of which 1 were waited for; matrix products, arithmetic and copies ran while one was open for 1% of the time, Pallas kernels for 0%

profile of v1, /device:TPU:0, one launch (start us, length us, event | category | flops | bytes accessed | tf_op | source)
XLA Modules:
  0.0 106.6 jit_solution(6374747203646818595)
XLA Ops:
  2.3 3.0 %fusion.10 = f32[2,1,80,128]{3,0,2,1:T(2,128)S(1)} fusion(s32[80,128]{1,0:T(8,128)S(1)} %get-tuple-element.16, bf16[2,80,128]{2,1,0:T(8,128)(2,1)} %bitcast.134), kind=kOutput, calls=%fused_computation.17 | convolution fusion | flops 6553600 | bytes 163840 | tf_op jit(solution)/shard_map/cbsk,skp->cbsp/dot_general | solution.py:31
  5.3 1.3 %fusion.45 = f32[80,480]{1,0:T(8,128)S(1)} fusion(f32[80,128]{1,0:T(8,128)S(1)} %bitcast.132, s32[128]{0:T(128)S(1)} %iota_add_fusion), kind=kOutput, calls=%fused_computation.70 | convolution fusion | flops 59535360 | bytes 195072 | tf_op jit(solution)/shard_map/bsp,pz->bsz/dot_general | solution.py:41
  6.7 1.4 %fusion.49 = f32[80,480]{1,0:T(8,128)S(1)} fusion(f32[80,128]{1,0:T(8,128)S(1)} %bitcast.133, s32[128]{0:T(128)S(1)} %iota_add_fusion), kind=kOutput, calls=%fused_computation.71 | convolution fusion | flops 59535360 | bytes 195072 | tf_op jit(solution)/shard_map/bsp,pz->bsz/dot_general | solution.py:44
  8.1 1.4 %fusion.9 = f32[1,1,80,480]{3,2,1,0:T(8,128)S(1)} fusion(f32[80,480]{1,0:T(8,128)S(1)} %fusion.45, f32[80,128]{1,0:T(8,128)S(1)} %bitcast.130, s32[128]{0:T(128)S(1)} %iota_add_fusion), kind=kOutput, calls=%fused_computation.16 | convolution fusion | flops 59573760 | bytes 348672 | tf_op jit(solution)/shard_map/bsp,pz->bsz/dot_general | solution.py:43
  9.5 1.4 %fusion.8 = f32[1,1,80,480]{3,2,1,0:T(8,128)S(1)} fusion(f32[80,480]{1,0:T(8,128)S(1)} %fusion.49, f32[80,128]{1,0:T(8,128)S(1)} %bitcast.131, s32[128]{0:T(128)S(1)} %iota_add_fusion), kind=kOutput, calls=%fused_computation.14 | convolution fusion | flops 59573760 | bytes 348672 | tf_op jit(solution)/shard_map/bsp,pz->bsz/dot_general | solution.py:46
  11.9 4.4 %all-to-all-start = ((f32[2,1,80,480]{2,1,0,3:T(1,128)}), f32[2,1,80,480]{2,1,0,3:T(1,128)S(1)}, u32[]{:S(2)}, u32[]{:S(2)}) async-start(f32[2,1,80,480]{2,1,0,3:T(1,128)} %copy.38), calls=%async_computation | async-start | bytes 983040 | tf_op jit(solution)/shard_map/all_to_all | solution.py:114
  16.4 24.4 %all-gather = bf16[32,1,80,128]{3,2,1,0:T(8,128)(2,1)S(1)} all-gather(bf16[2,1,80,128]{3,2,1,0:T(8,128)(2,1)S(1)} %copy.46), channel_id=2, replica_groups=mesh['band'=16,'ga'=2] {'band'}, dimensions={0}, use_global_device_ids=true | all-gather | bytes 696320 | tf_op jit(solution)/shard_map/all_gather | solution.py:128
  42.3 1.9 %fusion.32 = f32[240,480]{1,0:T(8,128)S(1)} fusion(f32[160,240]{1,0:T(8,128)S(1)} %bitcast.128, f32[160]{0:T(256)S(1)} %compare_convert_fusion, s32[160]{0:T(256)S(1)} %broadcast_add_fusion), kind=kOutput, calls=%fused_computation.59 | convolution fusion | flops 221952000 | bytes 615680 | tf_op jit(solution)/shard_map/bsz,sx->bzx/dot_general | solution.py:51
  44.2 1.9 %fusion.33 = f32[240,480]{1,0:T(8,128)S(1)} fusion(f32[160,240]{1,0:T(8,128)S(1)} %bitcast.129, f32[160]{0:T(256)S(1)} %compare_convert_fusion, s32[160]{0:T(256)S(1)} %broadcast_add_fusion), kind=kOutput, calls=%fused_computation.60 | convolution fusion | flops 221952000 | bytes 615680 | tf_op jit(solution)/shard_map/bsz,sx->bzx/dot_general | solution.py:54
  46.1 1.9 %fusion.5 = f32[240,480]{1,0:T(8,128)S(1)} fusion(f32[240,480]{1,0:T(8,128)S(1)} %copy-done, f32[240,480]{1,0:T(8,128)S(1)} %fusion.32, f32[160,240]{1,0:T(8,128)S(1)} %bitcast.123, f32[160]{0:T(256)S(1)} %compare_convert_fusion, s32[160]{0:T(256)S(1)} %broadcast_add_fusion), kind=kOutput, calls=%fused_computation.8 | convolution fusion | flops 222182400 | bytes 1537280 | tf_op jit(solution)/shard_map/bsz,sx->bzx/dot_general | solution.py:53
  48.0 1.9 %fusion.31 = f32[160,240]{1,0:T(8,128)S(1)} fusion(f32[240,480]{1,0:T(8,128)S(1)} %fusion.5, f32[160]{0:T(256)S(1)} %compare_convert_fusion, s32[160]{0:T(256)S(1)} %broadcast_add_fusion), kind=kOutput, calls=%fused_computation.58 | convolution fusion | flops 221952000 | bytes 615680 | tf_op jit(solution)/shard_map/bzx,sx->bsz/dot_general | solution.py:59
  49.9 1.9 %fusion.4 = f32[240,480]{1,0:T(8,128)S(1)} fusion(f32[240,480]{1,0:T(8,128)S(1)} %copy-done, f32[240,480]{1,0:T(8,128)S(1)} %fusion.33, f32[160,240]{1,0:T(8,128)S(1)} %bitcast.124, f32[160]{0:T(256)S(1)} %compare_convert_fusion, s32[160]{0:T(256)S(1)} %broadcast_add_fusion), kind=kOutput, calls=%fused_computation.6 | convolution fusion | flops 222182400 | bytes 1537280 | tf_op jit(solution)/shard_map/bsz,sx->bzx/dot_general | solution.py:56
  51.8 1.9 %fusion.30 = f32[160,240]{1,0:T(8,128)S(1)} fusion(f32[240,480]{1,0:T(8,128)S(1)} %fusion.4, f32[160]{0:T(256)S(1)} %compare_convert_fusion, s32[160]{0:T(256)S(1)} %broadcast_add_fusion), kind=kOutput, calls=%fused_computation.57 | convolution fusion | flops 221952000 | bytes 615680 | tf_op jit(solution)/shard_map/bzx,sx->bsz/dot_general | solution.py:62
  53.7 2.1 %fusion.7 = f32[1,1,160,240]{3,2,1,0:T(8,128)S(1)} fusion(f32[160,240]{1,0:T(8,128)S(1)} %fusion.31, f32[240,480]{1,0:T(8,128)S(1)} %fusion.4, f32[160]{0:T(256)S(1)} %compare_convert_fusion, s32[160]{0:T(256)S(1)} %broadcast_add_fusion), kind=kOutput, calls=%fused_computation.12 | convolution fusion | flops 221990400 | bytes 769280 | tf_op jit(solution)/shard_map/bzx,sx->bsz/dot_general | solution.py:61
  55.9 1.9 %fusion.6 = f32[1,1,160,240]{3,2,1,0:T(8,128)S(1)} fusion(f32[160,240]{1,0:T(8,128)S(1)} %fusion.30, f32[240,480]{1,0:T(8,128)S(1)} %fusion.5, f32[160]{0:T(256)S(1)} %compare_convert_fusion, s32[160]{0:T(256)S(1)} %broadcast_add_fusion), kind=kOutput, calls=%fused_computation.10 | convolution fusion | flops 221990400 | bytes 769280 | tf_op jit(solution)/shard_map/bzx,sx->bsz/dot_general | solution.py:64
  58.9 3.5 %all-to-all-start.1 = ((f32[2,1,160,240]{3,1,0,2:T(1,128)}), f32[2,1,160,240]{3,1,0,2:T(1,128)S(1)}, u32[]{:S(2)}, u32[]{:S(2)}) async-start(f32[2,1,160,240]{3,1,0,2:T(1,128)} %copy.42), calls=%async_computation.1 | async-start | bytes 655360 | tf_op jit(solution)/shard_map/all_to_all | solution.py:116
  62.8 6.5 %all-to-all-done.1 = f32[2,1,160,240]{3,1,0,2:T(1,128)S(1)} async-done(((f32[2,1,160,240]{3,1,0,2:T(1,128)}), f32[2,1,160,240]{3,1,0,2:T(1,128)S(1)}, u32[]{:S(2)}, u32[]{:S(2)}) %all-to-all-start.1) | async-done | bytes 307232 | tf_op jit(solution)/shard_map/all_to_all | solution.py:116
  70.0 1.4 %fusion.42 = f32[80,128]{1,0:T(8,128)S(1)} fusion(f32[80,480]{1,0:T(8,128)S(1)} %reshape.289, s32[128]{0:T(128)S(1)} %iota_add_fusion), kind=kOutput, calls=%fused_computation.69 | convolution fusion | flops 59535360 | bytes 195072 | tf_op jit(solution)/shard_map/bsz,pz->bsp/dot_general | solution.py:69
  71.6 1.4 %fusion.40 = f32[80,128]{1,0:T(8,128)S(1)} fusion(f32[80,480]{1,0:T(8,128)S(1)} %reshape.290, s32[128]{0:T(128)S(1)} %iota_add_fusion), kind=kOutput, calls=%fused_computation.68 | convolution fusion | flops 59535360 | bytes 195072 | tf_op jit(solution)/shard_map/bsz,pz->bsp/dot_general | solution.py:72
  73.0 1.4 %fusion.16 = f32[1,80,128]{2,1,0:T(8,128)S(1)} fusion(f32[80,128]{1,0:T(8,128)S(1)} %fusion.42, f32[80,480]{1,0:T(8,128)S(1)} %reshape.290, s32[128]{0:T(128)S(1)} %iota_add_fusion), kind=kOutput, calls=%fused_computation.25 | convolution fusion | flops 59545600 | bytes 236032 | tf_op jit(solution)/shard_map/bsz,pz->bsp/dot_general | solution.py:71
  74.5 1.5 %fusion.15 = f32[1,80,128]{2,1,0:T(8,128)S(1)} fusion(f32[80,128]{1,0:T(8,128)S(1)} %fusion.40, f32[80,480]{1,0:T(8,128)S(1)} %reshape.289, s32[128]{0:T(128)S(1)} %iota_add_fusion), kind=kOutput, calls=%fused_computation.23 | convolution fusion | flops 59545600 | bytes 236032 | tf_op jit(solution)/shard_map/bsz,pz->bsp/dot_general | solution.py:74
  76.0 5.6 %fusion.14 = bf16[2,1,80,128]{3,0,2,1:T(2,128)(2,1)S(1)} fusion(s32[80,128]{1,0:T(8,128)S(1)} %get-tuple-element.16, f32[2,80,128]{2,1,0:T(8,128)S(1)} %maximum_multiply_fusion, pred[80,128]{1,0:T(8,128)(4,1)S(1)} %broadcast_compare_fusion, f32[80,128]{1,0:T(8,128)S(1)} %get-tuple-element.15, bf16[2,1,80,128]{3,2,1,0:T(8,128)(2,1)S(1)} %copy-done.1), kind=kOutput, calls=%fused_computation.21 | convolution fusion | flops 32870400 | bytes 256000 | tf_op jit(solution)/shard_map/cbsp,skp->cbsk/dot_general | solution.py:35
  83.1 4.9 %psum.7 = f32[2,2,16,1]{2,3,1,0:T(1,128)S(1)} all-reduce(f32[2,2,16,1]{2,3,1,0:T(1,128)S(1)} %pad_maximum_fusion.2), channel_id=1, replica_groups=mesh['band'=16,'ga'=2] {'ga'}, use_global_device_ids=true, to_apply=%region_0.1 | all-reduce | flops 64 | bytes 512 | tf_op jit(solution)/shard_map/psum | solution.py:134
  88.1 17.2 %all_gather.11 = f32[2,2,16,16]{2,1,0,3:T(2,128)S(1)} all-gather(f32[2,2,16,1]{2,1,0,3:T(2,128)S(1)} %bitcast.135), channel_id=1, replica_groups=mesh['band'=16,'ga'=2] {'band'}, dimensions={3}, use_global_device_ids=true | all-gather | bytes 4352 | tf_op jit(solution)/shard_map/all_gather | solution.py:135
  (45 shorter events, 9.7 us)
Async XLA Ops:
  11.9 4.4 %copy-start.2 = (s32[160]{0:T(256)S(1)}, s32[160]{0:T(256)}, u32[]{:S(2)}) copy-start(s32[160]{0:T(256)} %param.6) | copy-start | bytes 1924
  11.9 4.4 %copy-start.1 = (bf16[2,1,80,128]{3,2,1,0:T(8,128)(2,1)S(1)}, bf16[2,1,80,128]{3,2,1,0:T(8,128)(2,1)}, u32[]{:S(2)}) copy-start(bf16[2,1,80,128]{3,2,1,0:T(8,128)(2,1)} %param.4) | copy-start | bytes 122884
  11.9 29.4 %all-to-all-start = ((f32[2,1,80,480]{2,1,0,3:T(1,128)}), f32[2,1,80,480]{2,1,0,3:T(1,128)S(1)}, u32[]{:S(2)}, u32[]{:S(2)}) async-start(f32[2,1,80,480]{2,1,0,3:T(1,128)} %copy.38), calls=%async_computation | async-start | bytes 983040 | tf_op jit(solution)/shard_map/all_to_all | solution.py:114
  44.2 1.9 %copy-start = (f32[240,480]{1,0:T(8,128)S(1)}, f32[240,480]{1,0:T(8,128)}, u32[]{:S(2)}) copy-start(f32[240,480]{1,0:T(8,128)} %param.5) | copy-start | bytes 1382404
  58.9 10.4 %all-to-all-start.1 = ((f32[2,1,160,240]{3,1,0,2:T(1,128)}), f32[2,1,160,240]{3,1,0,2:T(1,128)S(1)}, u32[]{:S(2)}, u32[]{:S(2)}) async-start(f32[2,1,160,240]{3,1,0,2:T(1,128)} %copy.42), calls=%async_computation.1 | async-start | bytes 655360 | tf_op jit(solution)/shard_map/all_to_all | solution.py:116
